TPU v7x, 32 devices: a whole 2x2x4 slice. The times are simulated.
32 devices in a mesh: ctx: 8 (over z, x), head: 4 (over y, core).
Axes of the slice: x: 2, y: 2, z: 4, core: 2. Of those that a mesh axis runs over, the one named last changes fastest.
Arguments:
- query_nope: bfloat16 [32, 16384], P('ctx', 'head'), may hold values from -15 to 15
- query_rope: bfloat16 [32, 8192], P('ctx', 'head'), may hold values from -8 to 8
- cache_latent: bfloat16 [512, 128, 512], P('ctx'), may hold values from -6 to 6
- cache_rope: bfloat16 [512, 8192], P('ctx'), may hold values from -8 to 8
- key_up: bfloat16 [128, 128, 512], P('head'), may hold values from -0.25 to 0.25
- value_up: bfloat16 [128, 512, 128], P('head'), may hold values from -0.25 to 0.25
- lengths: int32 [16], replicated, may hold values from 1024 to 4096, as said below
- block_owner: int32 [512], P('ctx'), may hold values from -1 to 15, as said below
- block_number: int32 [512], P('ctx'), may hold values from 0 to 31, as said below
Outputs:
- attended: bfloat16 [32, 16384], P('ctx', 'head')
Inputs may be any that keep to these rules, and one draw needn't show every extreme that they name: `lengths`: at least one sequence has exactly 4096 positions. A slot with block_owner -1 holds nothing. Sequence b owns exactly ceil(lengths[b] / 128) slots. The slots of sequence b carry block_number 0 to ceil(lengths[b] / 128) - 1, each once; empty slots carry 0.
All inputs are finite; a program needn't handle non-finite values.
Results may differ from a plain program's by a relative error of at most 0.023.
Values may be sent and summed in bfloat16 or wider, within the bound.
A program may use at most 128 MiB of HBM per device.

v0:
```python
import math

import jax
import jax.numpy as jnp
from jax import lax
from jax.sharding import PartitionSpec as P

score_scale = 192.0 ** (-0.5) * (1.0 + 0.1 * math.log(40.0)) ** 2
floor_value = -1e30


def joined(value, axis, join):
    pieces = jax.tree.map(lambda part: lax.all_gather(part, axis), value)
    head = jax.tree.map(lambda part: part[0], pieces)
    tail = jax.tree.map(lambda part: part[1:], pieces)
    total, _ = lax.scan(lambda total, slab: (join(total, slab), None), head, tail)
    return total


def combine_partials(earlier, later):
    new_top = jnp.maximum(earlier[0], later[0])
    scale_early = jnp.exp(earlier[0] - new_top)
    scale_late = jnp.exp(later[0] - new_top)
    row_total = earlier[1] * scale_early + later[1] * scale_late
    row_accum = earlier[2] * scale_early[..., None] + later[2] * scale_late[..., None]
    return (new_top, row_total, row_accum)


def per_device(
    query_nope,
    query_rope,
    cache_latent,
    cache_rope,
    key_up,
    value_up,
    lengths,
    block_owner,
    block_number,
):
    ctx_count = lax.axis_size("ctx")
    row_part = query_nope.shape[0]
    head_part = key_up.shape[0]
    nope_width = key_up.shape[1]
    latent_width = key_up.shape[2]
    value_width = value_up.shape[2]
    rope_width = query_rope.shape[1] // head_part
    rows_all = row_part * ctx_count
    seq_count = lengths.shape[0]
    new_tokens = rows_all // seq_count
    block_count = cache_latent.shape[0]
    block_width = cache_latent.shape[1]
    query_count = rows_all * head_part
    own_query = jnp.einsum(
        "rhn,hnc->rhc",
        query_nope.reshape(row_part, head_part, nope_width),
        key_up,
        preferred_element_type=jnp.float32,
    ).astype(jnp.bfloat16)
    own_rope = query_rope.reshape(row_part, head_part, rope_width)
    full_query, full_rope = (
        lax.all_gather(own_query, "ctx", axis=0, tiled=True),
        lax.all_gather(own_rope, "ctx", axis=0, tiled=True),
    )
    flat_query = full_query.reshape(query_count, latent_width)
    flat_rope = full_rope.reshape(query_count, rope_width)
    per_step = math.gcd(block_count, 32)
    turn_count = block_count // per_step
    key_count = per_step * block_width
    latent_sets = cache_latent.reshape(turn_count, key_count, latent_width)
    rope_sets = cache_rope.reshape(turn_count, key_count, rope_width)
    owner_sets = block_owner.reshape(turn_count, per_step)
    number_sets = block_number.reshape(turn_count, per_step)
    row_ids = jnp.arange(rows_all, dtype=jnp.int32)
    row_seq = row_ids // new_tokens
    row_limit = lengths[row_seq] - (new_tokens - 1 - row_ids % new_tokens)
    slot_ids = jnp.arange(block_width, dtype=jnp.int32)

    def attend(running, blockset):
        row_top, row_total, row_accum = running
        key_latent, rope_keys, owners, numbers = blockset
        logits = jnp.einsum("qc,kc->qk", flat_query, key_latent, preferred_element_type=jnp.float32)
        logits = logits + jnp.einsum(
            "qd,kd->qk", flat_rope, rope_keys, preferred_element_type=jnp.float32
        )
        logits = logits * score_scale
        key_owner = jnp.repeat(owners, block_width)
        key_position = (numbers[:, None] * block_width + slot_ids[None, :]).reshape(key_count)
        visible = (key_owner[None, :] == row_seq[:, None]) & (
            key_position[None, :] < row_limit[:, None]
        )
        visible = jnp.broadcast_to(visible[:, None, :], (rows_all, head_part, key_count)).reshape(
            query_count, key_count
        )
        logits = jnp.where(visible, logits, floor_value)
        new_top = jnp.maximum(row_top, jnp.max(logits, axis=1))
        weight = jnp.where(visible, jnp.exp(logits - new_top[:, None]), 0.0)
        part_total = jnp.sum(weight, axis=1)
        part_accum = jnp.dot(
            weight.astype(jnp.bfloat16), key_latent, preferred_element_type=jnp.float32
        )
        shrink = jnp.exp(row_top - new_top)
        return (new_top, row_total * shrink + part_total, row_accum * shrink[:, None] + part_accum)

    def advance(running, blockset):
        result = attend(running, blockset)
        return (result, None)

    starting = (
        jnp.full((query_count,), floor_value, jnp.float32),
        jnp.zeros((query_count,), jnp.float32),
        jnp.zeros((query_count, latent_width), jnp.float32),
    )
    running, unused = lax.scan(advance, starting, (latent_sets, rope_sets, owner_sets, number_sets))
    row_top = running[0].reshape(rows_all, head_part)
    row_total = running[1].reshape(rows_all, head_part)
    row_accum = running[2].reshape(rows_all, head_part, latent_width)
    value_real = value_up.astype(jnp.float32)
    row_start = lax.axis_index("ctx") * row_part
    merged = joined(
        (
            row_top,
            row_total,
            jnp.einsum("rhc,hcv->rhv", row_accum, value_real, precision=lax.Precision.HIGHEST),
        ),
        "ctx",
        combine_partials,
    )
    own_accum = lax.dynamic_slice_in_dim(merged[2], row_start, row_part, 0)
    own_total = lax.dynamic_slice_in_dim(merged[1], row_start, row_part, 0)
    attended = own_accum / own_total[:, :, None]
    return attended.astype(jnp.bfloat16).reshape(row_part, head_part * value_width)


def solution(mesh):
    return jax.shard_map(
        per_device,
        mesh=mesh,
        in_specs=(
            P("ctx", "head"),
            P("ctx", "head"),
            P("ctx", None, None),
            P("ctx", None),
            P("head", None, None),
            P("head", None, None),
            P(),
            P("ctx"),
            P("ctx"),
        ),
        out_specs=P("ctx", "head"),
        check_vma=False,
    )
```

profile of v0, /device:TPU:0, one launch (start us, length us, event | category | flops | bytes accessed | tf_op | source)
XLA Modules:
  0.0 268.8 jit_solution(15041405106024903679)
XLA Ops:
  7.3 2.8 %fusion.40 = bf16[4,32,512]{2,0,1:T(4,128)(2,1)S(1)} fusion(bf16[32,128,512]{2,1,0:T(8,128)(2,1)} %param.17, bf16[4,4096]{1,0:T(4,128)(2,1)S(1)} %copy-done), kind=kOutput, calls=%fused_computation.54 | convolution fusion | flops 16842752 | bytes 4358144 | tf_op jit(solution)/shard_map/rhn,hnc->rhc/dot_general | solution.py:53
  10.9 2.3 reshape.163
  13.5 0.7 gather_fusion
  14.2 33.1 %all_gather.19 = bf16[32,32,64]{2,1,0:T(8,128)(2,1)S(1)} all-gather(bf16[4,32,64]{2,1,0:T(8,128)(2,1)S(1)} %reshape.164), channel_id=1, replica_groups=mesh['ctx'=8,'head'=4] {'ctx'}, dimensions={0}, use_global_device_ids=true | all-gather | bytes 147456 | tf_op jit(solution)/shard_map/all_gather | solution.py:62
  47.3 7.6 %all-gather.4.cloned.1.call-done = bf16[32,32,512]{2,1,0:T(8,128)(2,1)} async-done(((bf16[4,32,512]{2,1,0:T(8,128)(2,1)}), bf16[32,32,512]{2,1,0:T(8,128)(2,1)}) %all-gather.4.cloned.1.call-update) | async-done | bytes 1048592 | tf_op jit(solution)/shard_map/all_gather | solution.py:61
  54.9 108.2 %while.30 = (s32[]{:T(128)}, f32[1024]{0:T(1024)S(1)}, f32[1024]{0:T(1024)S(1)}, f32[1024,512]{1,0:T(8,128)}, s32[2,32]{1,0:T(2,128)S(1)}, /*index=5*/s32[2,32]{...) while((s32[]{:T(128)}, f32[1024]{0:T(1024)S(1)}, ...), condition=%wide.region_3.4_spmd.clone, body=%wide.region_0.3_spmd.clone.sunk | while | flops 9170724864 | bytes 178915184 | solution.py:113
  55.3 1.1 broadcast_in_dim.58
  56.4 7.7 %copy.44 = pred[1024,4096]{0,1:T(32,128)(4,1)S(1)} copy(pred[1024,4096]{1,0:T(32,128)(4,1)S(1)} %bitcast.89) | data formatting | bytes 8388608 | tf_op jit(solution)/shard_map/while/body/eval_jaxpr/reshape | solution.py:91
  64.1 8.3 %fusion.75 = f32[4096,1024]{1,0:T(8,128)} fusion(bf16[1024,512]{1,0:T(8,128)(2,1)S(1)} %copy-done.7, bf16[2,4096,512]{2,1,0:T(8,128)(2,1)S(1)} %copy-done.6, s32[]{:T(128)} %get-tuple-element.367), kind=kOutput, calls=%fused_computation.21.clone.1 | convolution fusion | flops 4294967296 | bytes 22020100 | tf_op jit(solution)/shard_map/while/body/eval_jaxpr/qc,kc->qk/dot_general | solution.py:81
  72.4 11.0 %fusion.76 = (f32[1024]{0:T(1024)S(1)}, f32[1024,4096]{0,1:T(8,128)}) fusion(pred[1024,4096]{0,1:T(32,128)(4,1)S(1)} %copy.44, f32[4096,1024]{1,0:T(8,128)} %fusion.75, bf16[1024,64]{1,0:T(8,128)(2,1)S(1)} %get-tuple-element.390, bf16[2,4096,64]{2,1,0:T(8,128)(2,1)S(1)} %get-tuple-element.389, s32[]{:T(128)} %get-tuple-element.367), kind=kOutput, calls=%fused_computation.72.clone.1 | convolution fusion | flops 553647104 | bytes 39063556 | tf_op jit(solution)/shard_map/while/body/eval_jaxpr/qd,kd->qk/dot_general | solution.py:82
  83.4 11.2 %fusion.77 = f32[1024]{0:T(1024)S(1)} fusion(pred[1024,4096]{0,1:T(32,128)(4,1)} %copy-done.2, f32[1024,4096]{0,1:T(8,128)} %get-tuple-element.351, f32[1024]{0:T(1024)S(1)} %select_maximum_fusion.2), kind=kLoop, calls=%fused_computation.16.clone.1 | loop fusion | flops 12581888 | bytes 20979712 | tf_op jit(solution)/shard_map/while/body/eval_jaxpr/reduce_sum | solution.py:97
  94.6 14.1 %fusion.79 = f32[1024,512]{1,0:T(8,128)} fusion(f32[1024,512]{1,0:T(8,128)} %get-tuple-element.370, bf16[2,4096,512]{2,1,0:T(8,128)(2,1)} %get-tuple-element.387, s32[]{:T(128)} %get-tuple-element.367, pred[1024,4096]{0,1:T(32,128)(4,1)} %copy-done.2, f32[1024,4096]{0,1:T(8,128)} %get-tuple-element.351, f32[1024]{0:T(1024)S(1)} %select_maximum_fusion.2, ...), kind=kOutput, calls=%fused_computation.26.clone.1 | convolution fusion | flops 4309123072 | bytes 29368832 | tf_op jit(solution)/shard_map/while/body/eval_jaxpr/dot_general | solution.py:98
  109.1 1.1 broadcast_in_dim.58
  110.2 7.7 %copy.44 = pred[1024,4096]{0,1:T(32,128)(4,1)S(1)} copy(pred[1024,4096]{1,0:T(32,128)(4,1)S(1)} %bitcast.89) | data formatting | bytes 8388608 | tf_op jit(solution)/shard_map/while/body/eval_jaxpr/reshape | solution.py:91
  117.9 8.3 %fusion.75 = f32[4096,1024]{1,0:T(8,128)} fusion(bf16[1024,512]{1,0:T(8,128)(2,1)S(1)} %copy-done.7, bf16[2,4096,512]{2,1,0:T(8,128)(2,1)S(1)} %copy-done.6, s32[]{:T(128)} %get-tuple-element.367), kind=kOutput, calls=%fused_computation.21.clone.1 | convolution fusion | flops 4294967296 | bytes 22020100 | tf_op jit(solution)/shard_map/while/body/eval_jaxpr/qc,kc->qk/dot_general | solution.py:81
  126.2 11.0 %fusion.76 = (f32[1024]{0:T(1024)S(1)}, f32[1024,4096]{0,1:T(8,128)}) fusion(pred[1024,4096]{0,1:T(32,128)(4,1)S(1)} %copy.44, f32[4096,1024]{1,0:T(8,128)} %fusion.75, bf16[1024,64]{1,0:T(8,128)(2,1)S(1)} %get-tuple-element.390, bf16[2,4096,64]{2,1,0:T(8,128)(2,1)S(1)} %get-tuple-element.389, s32[]{:T(128)} %get-tuple-element.367), kind=kOutput, calls=%fused_computation.72.clone.1 | convolution fusion | flops 553647104 | bytes 39063556 | tf_op jit(solution)/shard_map/while/body/eval_jaxpr/qd,kd->qk/dot_general | solution.py:82
  137.2 11.2 %fusion.77 = f32[1024]{0:T(1024)S(1)} fusion(pred[1024,4096]{0,1:T(32,128)(4,1)} %copy-done.2, f32[1024,4096]{0,1:T(8,128)} %get-tuple-element.351, f32[1024]{0:T(1024)S(1)} %select_maximum_fusion.2), kind=kLoop, calls=%fused_computation.16.clone.1 | loop fusion | flops 12581888 | bytes 20979712 | tf_op jit(solution)/shard_map/while/body/eval_jaxpr/reduce_sum | solution.py:97
  148.4 14.7 %fusion.79 = f32[1024,512]{1,0:T(8,128)} fusion(f32[1024,512]{1,0:T(8,128)} %get-tuple-element.370, bf16[2,4096,512]{2,1,0:T(8,128)(2,1)} %get-tuple-element.387, s32[]{:T(128)} %get-tuple-element.367, pred[1024,4096]{0,1:T(32,128)(4,1)} %copy-done.2, f32[1024,4096]{0,1:T(8,128)} %get-tuple-element.351, f32[1024]{0:T(1024)S(1)} %select_maximum_fusion.2, ...), kind=kOutput, calls=%fused_computation.26.clone.1 | convolution fusion | flops 4309123072 | bytes 29368832 | tf_op jit(solution)/shard_map/while/body/eval_jaxpr/dot_general | solution.py:98
  163.1 6.4 %fusion.37 = f32[32,32,128]{2,0,1:T(8,128)} fusion(bf16[32,512,128]{2,1,0:T(8,128)(2,1)} %param.18, f32[32,32,512]{2,1,0:T(8,128)} %bitcast.92), kind=kOutput, calls=%fused_computation.52 | convolution fusion | flops 805306368 | bytes 6815744 | tf_op jit(solution)/shard_map/rhc,hcv->rhv/dot_general | solution.py:123
  169.6 31.6 %all_gather.20 = f32[8,32,32]{2,1,0:T(8,128)S(1)} all-gather(f32[1,32,32]{2,1,0:T(8,128)S(1)} %all_gather_reshape.6), channel_id=1, replica_groups=mesh['ctx'=8,'head'=4] {'ctx'}, dimensions={0}, use_global_device_ids=true | all-gather | bytes 36864 | tf_op jit(solution)/shard_map/all_gather | solution.py:13
  201.3 31.9 %all_gather.21 = f32[8,32,32]{2,1,0:T(8,128)S(1)} all-gather(f32[1,32,32]{2,1,0:T(8,128)S(1)} %all_gather_reshape.7), channel_id=1, replica_groups=mesh['ctx'=8,'head'=4] {'ctx'}, dimensions={0}, use_global_device_ids=true | all-gather | bytes 36864 | tf_op jit(solution)/shard_map/all_gather | solution.py:13
  233.2 10.5 %all-gather.6.cloned.1.call-done = f32[256,32,128]{2,0,1:T(8,128)} async-done(((f32[32,32,128]{2,0,1:T(8,128)}), f32[256,32,128]{2,0,1:T(8,128)}) %all-gather.6.cloned.1.call-update) | async-done | bytes 4194320 | tf_op jit(solution)/shard_map/all_gather | solution.py:13
  243.7 1.1 slice.30
  245.1 4.1 %slice.33 = f32[224,32,128]{2,0,1:T(8,128)} slice(f32[256,32,128]{2,0,1:T(8,128)} %all-gather.6.cloned.1.call-done), slice={[32:256], [0:32], [0:128]} | slice | bytes 7340032 | tf_op jit(solution)/shard_map/slice | solution.py:15
  249.2 12.0 %while.29 = (s32[]{:T(128)}, f32[32,32]{1,0:T(8,128)S(1)}, f32[32,32]{1,0:T(8,128)S(1)}, f32[32,32,128]{2,1,0:T(8,128)S(1)}, f32[7,32,32]{2,1,0:T(8,128)S(1)}, /...) while((s32[]{:T(128)}, f32[32,32]{1,0:T(8,128)S(1)}, f32[32,32]{1,0:T(8,128)S(1)}, ...), condition=%wide.region_5.6_spmd, body=%wide.region_4.5_spmd.sunk | while | flops 399362 | bytes 2662493 | solution.py:16
  249.2 1.1 constant_dynamic-slice_fusion.5
  250.9 1.1 constant_dynamic-slice_fusion.5
  252.6 1.1 constant_dynamic-slice_fusion.5
  254.4 1.1 constant_dynamic-slice_fusion.5
  256.1 1.1 constant_dynamic-slice_fusion.5
  257.8 1.1 constant_dynamic-slice_fusion.5
  259.5 1.1 constant_dynamic-slice_fusion.5
  (80 shorter events, 7.9 us)
Async XLA Ops:
  6.5 0.8 copy-start
  6.5 4.4 %copy-start.4 = (bf16[64,8192]{1,0:T(8,128)(2,1)S(1)}, bf16[64,8192]{1,0:T(8,128)(2,1)}, u32[]{:S(2)}) copy-start(bf16[64,8192]{1,0:T(8,128)(2,1)} %param.16) | copy-start | bytes 3145732
  6.5 6.7 %copy-start.5 = (bf16[4,2048]{1,0:T(4,128)(2,1)S(1)}, bf16[4,2048]{1,0:T(4,128)(2,1)}, u32[]{:S(2)}) copy-start(bf16[4,2048]{1,0:T(4,128)(2,1)} %param.14) | copy-start | bytes 49156
  6.5 6.8 %copy-start.8 = (s32[64]{0:T(128)S(1)}, s32[64]{0:T(128)}, u32[]{:S(2)}) copy-start(s32[64]{0:T(128)} %param.20) | copy-start | bytes 772
  6.5 6.9 %copy-start.9 = (s32[64]{0:T(128)S(1)}, s32[64]{0:T(128)}, u32[]{:S(2)}) copy-start(s32[64]{0:T(128)} %param.21) | copy-start | bytes 772
  6.5 7.0 %copy-start.3 = (s32[16]{0:T(128)S(1)}, s32[16]{0:T(128)}, u32[]{:S(2)}) copy-start(s32[16]{0:T(128)} %param.19) | copy-start | bytes 196
  6.6 48.4 %all-gather.4.cloned.1.call-start = ((), (), s32[]{:S(2)}) async-start(), calls=%async_computation | async-start | bytes 1179648 | tf_op jit(solution)/shard_map/all_gather | solution.py:61
  10.8 232.9 %all-gather.6.cloned.1.call-start = ((), (), s32[]{:S(2)}) async-start(), calls=%async_computation.1 | async-start | bytes 4718592 | tf_op jit(solution)/shard_map/all_gather | solution.py:13
  55.3 8.9 %copy-start.7 = (bf16[1024,512]{1,0:T(8,128)(2,1)S(1)}, bf16[1024,512]{1,0:T(8,128)(2,1)}, u32[]{:S(2)}) copy-start(bf16[1024,512]{1,0:T(8,128)(2,1)} %get-tuple-element.388) | copy-start | bytes 3145732 | tf_op jit(solution)/shard_map/while
  56.4 7.8 %copy-start.6 = (bf16[2,4096,512]{2,1,0:T(8,128)(2,1)S(1)}, bf16[2,4096,512]{2,1,0:T(8,128)(2,1)}, u32[]{:S(2)}) copy-start(bf16[2,4096,512]{2,1,0:T(8,128)(2,1)} %get-tuple-element.387) | copy-start | bytes 25165828 | tf_op jit(solution)/shard_map/while
  64.1 8.3 %copy-start.2 = (pred[1024,4096]{0,1:T(32,128)(4,1)}, pred[1024,4096]{0,1:T(32,128)(4,1)S(1)}, u32[]{:S(2)}) copy-start(pred[1024,4096]{0,1:T(32,128)(4,1)S(1)} %copy.44) | copy-start | bytes 12582916 | tf_op jit(solution)/shard_map/while
  109.0 8.9 %copy-start.7 = (bf16[1024,512]{1,0:T(8,128)(2,1)S(1)}, bf16[1024,512]{1,0:T(8,128)(2,1)}, u32[]{:S(2)}) copy-start(bf16[1024,512]{1,0:T(8,128)(2,1)} %get-tuple-element.388) | copy-start | bytes 3145732 | tf_op jit(solution)/shard_map/while
  110.1 7.8 %copy-start.6 = (bf16[2,4096,512]{2,1,0:T(8,128)(2,1)S(1)}, bf16[2,4096,512]{2,1,0:T(8,128)(2,1)}, u32[]{:S(2)}) copy-start(bf16[2,4096,512]{2,1,0:T(8,128)(2,1)} %get-tuple-element.387) | copy-start | bytes 25165828 | tf_op jit(solution)/shard_map/while
  117.9 8.3 %copy-start.2 = (pred[1024,4096]{0,1:T(32,128)(4,1)}, pred[1024,4096]{0,1:T(32,128)(4,1)S(1)}, u32[]{:S(2)}) copy-start(pred[1024,4096]{0,1:T(32,128)(4,1)S(1)} %copy.44) | copy-start | bytes 12582916 | tf_op jit(solution)/shard_map/while
  249.2 12.8 %copy-start.1 = (bf16[4,4096]{1,0:T(4,128)(2,1)S(1)}, bf16[4,4096]{1,0:T(4,128)(2,1)}, u32[]{:S(2)}) copy-start(bf16[4,4096]{1,0:T(4,128)(2,1)} %param.13) | copy-start | bytes 98308
Sparse Core Ops, SparseCore 0:
  11.0 43.9 all-gather.3
  169.7 73.9 all-gather.5
where the time goes:
time: 269 us
  blocking collectives  96.5 us (36%)
  matrix products  76.6 us (28%)
  local copies, waits for them, and re-layouts  36.4 us (14%)
  other arithmetic  27.2 us (10%)
  waiting for transfers between devices  18.2 us (7%)
  between operations  13.6 us (5%)
    all_gather x2, blocking collectives, joined(): pieces = jax.tree.map(lambda part: lax.all_gather(part, axis), value)  63.4 us
    all_gather x1, blocking collectives, per_device(): lax.all_gather(own_rope, 'ctx', axis=0, tiled=True)  33.1 us
    dot_general x2, matrix products, attend(): jnp.dot(weight.astype(jnp.bfloat16), key_latent, preferred_element_type=j...  28.8 us
    reduce_sum x2, other arithmetic, attend(): part_total = jnp.sum(weight, axis=1)  22.4 us
    dot_general x2, matrix products, attend(): jnp.einsum('qd,kd->qk', flat_rope, rope_keys, preferred_element_type=jnp....  22 us
    dot_general x2, matrix products, attend(): jnp.einsum('qc,kc->qk', flat_query, key_latent, preferred_element_type=jn...  16.5 us
    reshape x2, local copies, waits for them, and re-layouts, attend(): jnp.broadcast_to(visible[:, None, :], (rows_all, head_part, key_count))  15.5 us
    all_gather x1, waiting for transfers between devices, joined(): pieces = jax.tree.map(lambda part: lax.all_gather(part, axis), value)  10.5 us
  transfers between devices with their start and end apart: 2, of which 2 were waited for; matrix products, arithmetic and copies ran while one was open for 1% of the time, Pallas kernels for 0%

commit v1 on v0

v1 whole, which is shorter than its diff:
```python
import functools
import math

import jax
import jax.numpy as jnp
from jax import lax
from jax.experimental import pallas as pl
from jax.experimental.pallas import tpu as pltpu
from jax.sharding import PartitionSpec as P

score_scale = 192.0 ** (-0.5) * (1.0 + 0.1 * math.log(40.0)) ** 2
floor_value = -1e30
LANES = 128
MESH = pl.DeviceIdType.MESH


def greet(count, me):
    barrier = pltpu.get_barrier_semaphore()
    for step in range(1, count):
        peer = lax.rem(me + step, count)
        pl.semaphore_signal(barrier, inc=1, device_id={"ctx": peer}, device_id_type=MESH)
    pl.semaphore_wait(barrier, count - 1)


def absorb_kernel(
    count, qn_ref, qr_ref, ku_hbm, q_ref, qn_all, qr_all, qn_wide, qr_wide, q_wide, ku,
    send_a, recv_a, send_b, recv_b, own_sem, ku_sem,
):
    me = lax.axis_index("ctx")
    heads = ku.shape[0]
    latent_tiles = ku.shape[2] // LANES
    row_part = qn_ref.shape[0]
    rows_all = row_part * count
    rope_width = qr_ref.shape[1] // heads
    weights = pltpu.make_async_copy(ku_hbm, ku, ku_sem)
    weights.start()
    own = [
        pltpu.make_async_copy(qn_ref, qn_all.at[me], own_sem.at[0]),
        pltpu.make_async_copy(qr_ref, qr_all.at[me], own_sem.at[1]),
    ]
    for copy in own:
        copy.start()
    greet(count, me)
    copies = []
    for step in range(1, count):
        peer = lax.rem(me + step, count)
        for src, dst, send_sem, recv_sem in (
            (qn_ref, qn_all, send_a, recv_a),
            (qr_ref, qr_all, send_b, recv_b),
        ):
            copy = pltpu.make_async_remote_copy(
                src_ref=src, dst_ref=dst.at[me], send_sem=send_sem.at[step],
                recv_sem=recv_sem.at[step], device_id={"ctx": peer}, device_id_type=MESH,
            )
            copy.start()
            copies.append(copy)
    for copy in own:
        copy.wait()
    for copy in copies:
        copy.wait()
    weights.wait()
    for source in range(count):
        rows = pl.ds(source * row_part, row_part)
        qn_wide[rows, :] = qn_all[source].astype(jnp.float32)
        qr_wide[rows, :] = qr_all[source].astype(jnp.float32)

    group = 4

    def one_group(turn, carry):
        for inner in range(group):
            head = turn * group + inner
            lanes = pl.ds(pl.multiple_of(head * LANES, LANES), LANES)
            query = qn_wide[:, lanes].astype(jnp.bfloat16)
            result = jnp.dot(query, ku[head], preferred_element_type=jnp.float32)
            for tile in range(latent_tiles):
                q_wide[tile, pl.ds(head, rows_all, stride=heads), :] = result[
                    :, tile * LANES : (tile + 1) * LANES
                ]
        return carry

    lax.fori_loop(0, heads // group, one_group, 0)
    low = lax.broadcasted_iota(jnp.int32, (rows_all, LANES), 1) < rope_width
    for pair in range(heads // 2):
        chunk = qr_wide[:, pair * LANES : (pair + 1) * LANES]
        turned = pltpu.roll(chunk, rope_width, 1)
        q_wide[latent_tiles, pl.ds(2 * pair, rows_all, stride=heads), :] = jnp.where(
            low, chunk, turned
        )
        q_wide[latent_tiles, pl.ds(2 * pair + 1, rows_all, stride=heads), :] = jnp.where(
            low, turned, chunk
        )
    for tile in range(latent_tiles + 1):
        q_ref[:, tile * LANES : (tile + 1) * LANES] = q_wide[tile].astype(jnp.bfloat16)


def attend_kernel(
    count, new_tokens, lengths, owners, numbers, q_ref, lat_hbm, rope_hbm, vu_hbm, out_ref,
    stat_ref, lat, rope, keys, scores, tops, totals, accum, values, vu, lat_sem, rope_sem, vu_sem,
):
    blocks, width, latent_width = lat.shape
    latent_tiles = latent_width // LANES
    heads = vu.shape[0]
    seq_rows = new_tokens * heads
    queries = q_ref.shape[0]
    rows_all = queries // heads
    dest_rows = queries // count
    sets = lat_sem.shape[0]
    per_set = blocks // sets
    rope_copy = pltpu.make_async_copy(rope_hbm, rope, rope_sem)
    rope_copy.start()

    def lat_copy(part):
        span = pl.ds(part * per_set, per_set)
        return pltpu.make_async_copy(lat_hbm.at[span], lat.at[span], lat_sem.at[part])

    for part in range(sets):
        lat_copy(part).start()
    vu_copy = pltpu.make_async_copy(vu_hbm, vu, vu_sem)
    vu_copy.start()
    tops[...] = jnp.full(tops.shape, floor_value, jnp.float32)
    totals[...] = jnp.zeros(totals.shape, jnp.float32)
    accum[...] = jnp.zeros(accum.shape, jnp.float32)
    rope_copy.wait()
    rope_width = rope.shape[1] // width
    low = lax.broadcasted_iota(jnp.int32, (blocks, LANES), 1) < rope_width

    def spread(pair, carry):
        lanes = pl.ds(pl.multiple_of(pair * LANES, LANES), LANES)
        chunk = rope[:, lanes].astype(jnp.float32)
        keys[pl.ds(2 * pair, blocks, stride=width), :] = jnp.where(low, chunk, 0.0)
        keys[pl.ds(2 * pair + 1, blocks, stride=width), :] = jnp.where(low, 0.0, chunk)
        return carry

    lax.fori_loop(0, width // 2, spread, 0, unroll=4)

    token = lax.broadcasted_iota(jnp.int32, (seq_rows, width), 0) // heads
    slot = lax.broadcasted_iota(jnp.int32, (seq_rows, width), 1)
    offset = slot - token
    contract_last = (((1,), (1,)), ((), ()))

    def score_one(block):
        owner = owners[block]
        safe = jnp.maximum(owner, 0)
        rows = pl.ds(pl.multiple_of(safe * seq_rows, seq_rows), seq_rows)
        low_key = keys[pl.ds(pl.multiple_of(block * width, width), width), :].astype(jnp.bfloat16)
        logits = lax.dot_general(
            q_ref[rows, :latent_width], lat[block], contract_last,
            preferred_element_type=jnp.float32,
        ) + lax.dot_general(
            q_ref[rows, latent_width:], low_key, contract_last, preferred_element_type=jnp.float32
        )
        limit = lengths[safe] - (new_tokens - 1) - numbers[block] * width
        limit = jnp.where(owner >= 0, limit, -width)
        logits = jnp.where(offset < limit, logits * score_scale, floor_value)
        return rows, logits

    def score_set(part, carry):
        lat_copy(part).wait()
        for inner in range(per_set):
            block = part * per_set + inner
            rows, logits = score_one(block)
            scores[block] = logits
            tops[rows, :] = jnp.maximum(tops[rows, :], logits)
        return carry

    lax.fori_loop(0, sets, score_set, 0)
    for row in range(0, queries, seq_rows):
        rows = pl.ds(row, seq_rows)
        top = jnp.max(tops[rows, :], axis=1, keepdims=True)
        tops[rows, :] = jnp.broadcast_to(jnp.maximum(top, 0.1 * floor_value), (seq_rows, LANES))

    def weigh_set(part, carry):
        for inner in range(per_set):
            block = part * per_set + inner
            safe = jnp.maximum(owners[block], 0)
            rows = pl.ds(pl.multiple_of(safe * seq_rows, seq_rows), seq_rows)
            weight = jnp.exp(scores[block] - tops[rows, :])
            totals[rows, :] += weight
            part_accum = jnp.dot(
                weight.astype(jnp.bfloat16), lat[block], preferred_element_type=jnp.float32
            )
            for tile in range(latent_tiles):
                accum[tile, rows, :] += part_accum[:, tile * LANES : (tile + 1) * LANES]
        return carry

    lax.fori_loop(0, sets, weigh_set, 0)
    vu_copy.wait()
    group = 4

    def lift(turn, carry):
        for inner in range(group):
            head = turn * group + inner
            picked = pl.ds(head, rows_all, stride=heads)
            result = jnp.zeros((rows_all, LANES), jnp.float32)
            whole = jnp.concatenate(
                [accum[tile, picked, :].astype(jnp.bfloat16) for tile in range(latent_tiles)],
                axis=1,
            )
            values[picked, :] = jnp.dot(whole, vu[head], preferred_element_type=jnp.float32)
        return carry

    lax.fori_loop(0, heads // group, lift, 0)
    for dest in range(count):
        rows = pl.ds(dest * dest_rows, dest_rows)
        total = jnp.sum(totals[rows, :], axis=1, keepdims=True)
        held = total > 0.0
        safe_total = jnp.where(held, total, 1.0)
        mass = jnp.where(held, tops[rows, :] + jnp.log(safe_total), floor_value)
        out_ref[dest] = (values[rows, :] * (1.0 / safe_total)).astype(jnp.bfloat16)
        stat_ref[dest] = jnp.transpose(mass)[: stat_ref.shape[1], :]


def merge_kernel(
    count, heads, out_ref, stat_ref, result_ref, outs, stats, merged,
    send_a, recv_a, send_b, recv_b, own_sem,
):
    me = lax.axis_index("ctx")
    row_part = result_ref.shape[0]
    own = [
        pltpu.make_async_copy(out_ref.at[me], outs.at[me], own_sem.at[0]),
        pltpu.make_async_copy(stat_ref.at[me], stats.at[me], own_sem.at[1]),
    ]
    for copy in own:
        copy.start()
    greet(count, me)
    copies = []
    for step in range(1, count):
        peer = lax.rem(me + step, count)
        for src, dst, send_sem, recv_sem in (
            (stat_ref, stats, send_b, recv_b),
            (out_ref, outs, send_a, recv_a),
        ):
            copy = pltpu.make_async_remote_copy(
                src_ref=src.at[peer], dst_ref=dst.at[me], send_sem=send_sem.at[step],
                recv_sem=recv_sem.at[step], device_id={"ctx": peer}, device_id_type=MESH,
            )
            copy.start()
            copies.append(copy)
    for copy in own:
        copy.wait()
    for copy in copies:
        copy.wait()
    columns = [jnp.transpose(stats[source]) for source in range(count)]
    top = functools.reduce(jnp.maximum, columns)
    parts = [jnp.exp(column - top) for column in columns]
    total = functools.reduce(jnp.add, parts)
    inverse = 1.0 / total
    sum_parts = None
    for source in range(count):
        piece = (parts[source] * inverse)[:, :1] * outs[source].astype(jnp.float32)
        sum_parts = piece if sum_parts is None else sum_parts + piece
    merged[...] = sum_parts
    for head in range(heads):
        result_ref[:, head * LANES : (head + 1) * LANES] = merged[
            pl.ds(head, row_part, stride=heads), :
        ].astype(jnp.bfloat16)


def per_device(
    query_nope, query_rope, cache_latent, cache_rope, key_up, value_up, lengths, block_owner,
    block_number,
):
    count = lax.axis_size("ctx")
    row_part = query_nope.shape[0]
    heads, nope_width, latent_width = key_up.shape
    value_width = value_up.shape[2]
    rows_all = row_part * count
    new_tokens = rows_all // lengths.shape[0]
    blocks, width, _ = cache_latent.shape
    queries = rows_all * heads
    q_width = latent_width + LANES
    latent_tiles = latent_width // LANES
    dest_rows = row_part * heads
    vmem = pl.BlockSpec(memory_space=pltpu.VMEM)
    smem = pl.BlockSpec(memory_space=pltpu.SMEM)
    hbm = pl.BlockSpec(memory_space=pl.ANY)
    dma = pltpu.SemaphoreType.DMA
    f32, bf16 = jnp.float32, jnp.bfloat16
    query = pl.pallas_call(
        functools.partial(absorb_kernel, count),
        name="absorb",
        out_shape=jax.ShapeDtypeStruct((queries, q_width), bf16),
        in_specs=[vmem, vmem, hbm],
        out_specs=vmem,
        scratch_shapes=[
            pltpu.VMEM((count,) + query_nope.shape, bf16),
            pltpu.VMEM((count,) + query_rope.shape, bf16),
            pltpu.VMEM((rows_all, query_nope.shape[1]), f32),
            pltpu.VMEM((rows_all, query_rope.shape[1]), f32),
            pltpu.VMEM((latent_tiles + 1, queries, LANES), f32),
            pltpu.VMEM(key_up.shape, bf16),
            dma((count,)), dma((count,)), dma((count,)), dma((count,)), dma((2,)), dma,
        ],
        compiler_params=pltpu.CompilerParams(
            collective_id=0, has_side_effects=True, vmem_limit_bytes=24 * 1024 * 1024
        ),
    )(query_nope, query_rope, key_up)
    sets = 8
    outs, stats = pl.pallas_call(
        functools.partial(attend_kernel, count, new_tokens),
        name="attend",
        out_shape=(
            jax.ShapeDtypeStruct((count, dest_rows, value_width), bf16),
            jax.ShapeDtypeStruct((count, 8, dest_rows), f32),
        ),
        in_specs=[smem, smem, smem, vmem, hbm, hbm, hbm],
        out_specs=(vmem, vmem),
        scratch_shapes=[
            pltpu.VMEM(cache_latent.shape, bf16),
            pltpu.VMEM(cache_rope.shape, bf16),
            pltpu.VMEM((blocks * width, LANES), f32),
            pltpu.VMEM((blocks, new_tokens * heads, width), f32),
            pltpu.VMEM((queries, LANES), f32),
            pltpu.VMEM((queries, LANES), f32),
            pltpu.VMEM((latent_tiles, queries, LANES), f32),
            pltpu.VMEM((queries, LANES), f32),
            pltpu.VMEM(value_up.shape, bf16),
            dma((sets,)), dma, dma,
        ],
        compiler_params=pltpu.CompilerParams(vmem_limit_bytes=48 * 1024 * 1024),
    )(lengths, block_owner, block_number, query, cache_latent, cache_rope, value_up)
    return pl.pallas_call(
        functools.partial(merge_kernel, count, heads),
        name="merge",
        out_shape=jax.ShapeDtypeStruct((row_part, heads * value_width), bf16),
        in_specs=[vmem, vmem],
        out_specs=vmem,
        scratch_shapes=[
            pltpu.VMEM((count, dest_rows, value_width), bf16),
            pltpu.VMEM((count, 8, dest_rows), f32),
            pltpu.VMEM((dest_rows, LANES), f32),
            dma((count,)), dma((count,)), dma((count,)), dma((count,)), dma((2,)),
        ],
        compiler_params=pltpu.CompilerParams(
            collective_id=1, has_side_effects=True, vmem_limit_bytes=16 * 1024 * 1024
        ),
    )(outs, stats)


def solution(mesh):
    return jax.shard_map(
        per_device,
        mesh=mesh,
        in_specs=(
            P("ctx", "head"),
            P("ctx", "head"),
            P("ctx", None, None),
            P("ctx", None),
            P("head", None, None),
            P("head", None, None),
            P(),
            P("ctx"),
            P("ctx"),
        ),
        out_specs=P("ctx", "head"),
        check_vma=False,
    )
```

time: 269 us -> 50.3 us (0.19)
  blocking collectives: 96.5 us -> 0 us
  matrix products: 76.6 us -> 0 us
  Pallas kernels: 0 us -> 45.7 us
  local copies, waits for them, and re-layouts: 36.4 us -> 4.29 us
  other arithmetic: 27.2 us -> 0 us
  waiting for transfers between devices: 18.2 us -> 0 us
  between operations: 13.6 us -> 0.06 us
    all_gather x3 -> x0, blocking collectives: 96.5 us -> none  [the longest x2 63.4 us: joined(): pieces = jax.tree.map(lambda part: lax.all_gather(part, axis), value)]
    dot_general x8 -> x0, matrix products: 76.6 us -> none  [the longest x2 28.8 us: attend(): jnp.dot(weight.astype(jnp.bfloat16), key_latent, preferred_element_type=j...]
    pallas_call x0 -> x3, Pallas kernels: none -> 45.7 us  [the longest x1 17 us: per_device(): pl.pallas_call(functools.partial(absorb_kernel, count), name='absorb', ou...]
    reduce_sum x2 -> x0, other arithmetic: 22.4 us -> none  [attend(): part_total = jnp.sum(weight, axis=1)]
    all_gather x2 -> x0, waiting for transfers between devices: 18.1 us -> none  [the longest x1 10.5 us: joined(): pieces = jax.tree.map(lambda part: lax.all_gather(part, axis), value)]
    reshape x6 -> x0, local copies, waits for them, and re-layouts: 18 us -> none  [the longest x2 15.5 us: attend(): jnp.broadcast_to(visible[:, None, :], (rows_all, head_part, key_count))]
    dynamic_slice x8 -> x0, local copies, waits for them, and re-layouts: 7.65 us -> none  [the longest x7 7.63 us: joined(): lax.scan(lambda total, slab: (join(total, slab), None), head, tail)]
    slice x4 -> x0, local copies, waits for them, and re-layouts: 5.18 us -> none  [the longest x3 4.1 us: joined(): tail = jax.tree.map(lambda part: part[1:], pieces)]
  transfers between devices with their start and end apart: 2 -> 0, of which waited for: 2 -> 0; matrix products, arithmetic and copies ran while one was open for 1% -> 0% of each run, Pallas kernels for 0% -> 0%
where the time goes in v1:
time: 50.3 us; the launch traced here: 50 us
  Pallas kernels  45.7 us (91%)
  local copies, waits for them, and re-layouts  4.29 us (9%)
    pallas_call x1, Pallas kernels, per_device(): pl.pallas_call(functools.partial(absorb_kernel, count), name='absorb', ou...  17 us
    pallas_call x1, Pallas kernels, per_device(): pl.pallas_call(functools.partial(attend_kernel, count, new_tokens), name=...  16.3 us
    pallas_call x1, Pallas kernels, per_device(): pl.pallas_call(functools.partial(merge_kernel, count, heads), name='merge...  12.4 us
    unnamed x15, local copies, waits for them, and re-layouts  4.29 us

profile of v1, /device:TPU:0, one launch (start us, length us, event | category | flops | bytes accessed | tf_op | source)
XLA Modules:
  0.0 50.0 jit_solution(563509031904344652)
XLA Ops:
  0.0 0.0 copy-start
  0.0 2.2 %copy-done = bf16[32,128,512]{2,1,0:T(8,128)(2,1)S(1)} copy-done((bf16[32,128,512]{2,1,0:T(8,128)(2,1)S(1)}, bf16[32,128,512]{2,1,0:T(8,128)(2,1)}, u32[]{:S(2)}) %copy-start) | copy-done | bytes 4194328
  2.2 0.0 copy-start.2
  2.2 0.8 %copy-done.2 = bf16[4,4096]{1,0:T(4,128)(2,1)S(1)} copy-done((bf16[4,4096]{1,0:T(4,128)(2,1)S(1)}, bf16[4,4096]{1,0:T(4,128)(2,1)}, u32[]{:S(2)}) %copy-start.2) | copy-done | bytes 32792
  2.9 0.0 copy-start.3
  2.9 0.7 %copy-done.3 = bf16[4,2048]{1,0:T(4,128)(2,1)S(1)} copy-done((bf16[4,2048]{1,0:T(4,128)(2,1)S(1)}, bf16[4,2048]{1,0:T(4,128)(2,1)}, u32[]{:S(2)}) %copy-start.3) | copy-done | bytes 16408
  3.7 0.0 copy-start.1
  3.7 0.0 copy-start.4
  3.7 0.0 copy-start.5
  3.7 0.0 copy-start.6
  3.7 17.0 %absorb.1.q_ref = bf16[1024,640]{1,0:T(8,128)(2,1)S(1)} custom-call(bf16[4,4096]{1,0:T(4,128)(2,1)S(1)} %copy-done.2, bf16[4,2048]{1,0:T(4,128)(2,1)S(1)} %copy-done.3, bf16[32,128,512]{2,1,0:T(8,128)(2,1)S(1)} %copy-done), custom_call_target="tpu_custom_call" | custom-call | tf_op jit(solution)/shard_map/absorb/pallas_call | solution.py:279
  20.6 0.0 copy-done.1
  20.7 0.0 copy-done.4
  20.7 0.0 copy-done.5
  20.7 0.0 copy-done.6
  20.7 16.3 %attend.1 = (bf16[8,128,128]{2,1,0:T(8,128)(2,1)S(1)}, f32[8,8,128]{2,1,0:T(8,128)S(1)}) custom-call(s32[16]{0:T(128)S(1)} %copy-done.4, s32[64]{0:T(128)S(1)} %copy-done.5, s32[64]{0:T(128)S(1)} %copy-done.6, bf16[1024,640]{1,0:T(8,128)(2,1)S(1)} %absorb.1.q_ref, bf16[64,128,512]{2,1,0:T(8,128)(2,1)} %lat_hbm.1, bf16[64,8192]{1,0:T(8,128)(2,1)S(1)} %copy-done.1, ...), custom_call_target="tpu_custom_call" | custom-call | tf_op jit(solution)/shard_map/attend/pallas_call | solution.py:299
  37.0 12.4 %merge.1 = bf16[4,4096]{1,0:T(4,128)(2,1)S(1)} custom-call(bf16[8,128,128]{2,1,0:T(8,128)(2,1)S(1)} %get-tuple-element.7.out_ref, f32[8,8,128]{2,1,0:T(8,128)S(1)} %get-tuple-element.8.stat_ref), custom_call_target="tpu_custom_call" | custom-call | tf_op jit(solution)/shard_map/merge/pallas_call | solution.py:322
  49.4 0.6 %copy.11 = bf16[4,4096]{1,0:T(4,128)(2,1)} copy(bf16[4,4096]{1,0:T(4,128)(2,1)S(1)} %merge.1) | data formatting | bytes 65536
Async XLA Ops:
  0.0 2.2 %copy-start = (bf16[32,128,512]{2,1,0:T(8,128)(2,1)S(1)}, bf16[32,128,512]{2,1,0:T(8,128)(2,1)}, u32[]{:S(2)}) copy-start(bf16[32,128,512]{2,1,0:T(8,128)(2,1)} %ku_hbm.1) | copy-start | bytes 12582916
  2.2 0.8 %copy-start.2 = (bf16[4,4096]{1,0:T(4,128)(2,1)S(1)}, bf16[4,4096]{1,0:T(4,128)(2,1)}, u32[]{:S(2)}) copy-start(bf16[4,4096]{1,0:T(4,128)(2,1)} %qn_ref.1) | copy-start | bytes 98308
  2.9 0.7 %copy-start.3 = (bf16[4,2048]{1,0:T(4,128)(2,1)S(1)}, bf16[4,2048]{1,0:T(4,128)(2,1)}, u32[]{:S(2)}) copy-start(bf16[4,2048]{1,0:T(4,128)(2,1)} %qr_ref.1) | copy-start | bytes 49156
  3.7 17.0 %copy-start.1 = (bf16[64,8192]{1,0:T(8,128)(2,1)S(1)}, bf16[64,8192]{1,0:T(8,128)(2,1)}, u32[]{:S(2)}) copy-start(bf16[64,8192]{1,0:T(8,128)(2,1)} %rope_hbm.1) | copy-start | bytes 3145732
  3.7 17.0 %copy-start.4 = (s32[16]{0:T(128)S(1)}, s32[16]{0:T(128)}, u32[]{:S(2)}) copy-start(s32[16]{0:T(128)} %lengths.1) | copy-start | bytes 196
  3.7 17.0 %copy-start.5 = (s32[64]{0:T(128)S(1)}, s32[64]{0:T(128)}, u32[]{:S(2)}) copy-start(s32[64]{0:T(128)} %owners.1) | copy-start | bytes 772
  3.7 17.0 %copy-start.6 = (s32[64]{0:T(128)S(1)}, s32[64]{0:T(128)}, u32[]{:S(2)}) copy-start(s32[64]{0:T(128)} %numbers.1) | copy-start | bytes 772

commit v2 on v1

v2 whole, which is shorter than its diff:
```python
import functools
import math

import jax
import jax.numpy as jnp
from jax import lax
from jax.experimental import pallas as pl
from jax.experimental.pallas import tpu as pltpu
from jax.sharding import PartitionSpec as P

score_scale = 192.0 ** (-0.5) * (1.0 + 0.1 * math.log(40.0)) ** 2
floor_value = -1e30
LANES = 128
MESH = pl.DeviceIdType.MESH


def greet(count, me):
    barrier = pltpu.get_barrier_semaphore()
    for step in range(1, count):
        peer = lax.rem(me + step, count)
        pl.semaphore_signal(barrier, inc=1, device_id={"ctx": peer}, device_id_type=MESH)
    pl.semaphore_wait(barrier, count - 1)


def remote(src, dst, send_sem, recv_sem, peer):
    return pltpu.make_async_remote_copy(
        src_ref=src, dst_ref=dst, send_sem=send_sem, recv_sem=recv_sem,
        device_id={"ctx": peer}, device_id_type=MESH,
    )


def absorb_kernel(
    count, groups, qn_hbm, qr_hbm, ku_hbm, lat_hbm, rope_hbm, vu_hbm, q_ref, lat_a, lat_b,
    lat_c, lat_d, key_ref, vu_ref, qn_all, qr_all, qn_wide, qr_wide, q_wide, ku, rope, keys,
    send_z, recv_z, send_x, recv_x, own_sem, load_sem,
):
    me = lax.axis_index("ctx")
    outer = count // 2
    line, side = me // 2, lax.rem(me, 2)
    partner = me + 1 - 2 * side
    heads = ku.shape[0]
    latent_tiles = ku.shape[2] // LANES
    row_part = qn_hbm.shape[0]
    rows_all = row_part * count
    rope_width = qr_hbm.shape[1] // heads
    blocks = rope.shape[0]
    width = key_ref.shape[0] // blocks
    group_heads = heads // groups
    span = group_heads * LANES
    own = [
        pltpu.make_async_copy(
            qn_hbm.at[:, pl.ds(part * span, span)], qn_all.at[part, me], own_sem.at[part]
        )
        for part in range(groups)
    ] + [pltpu.make_async_copy(qr_hbm, qr_all.at[me], own_sem.at[groups])]
    lat_refs = (lat_a, lat_b, lat_c, lat_d)
    quarter = blocks // len(lat_refs)
    lat_parts = [
        (lat_hbm.at[pl.ds(place * quarter, quarter)], ref) for place, ref in enumerate(lat_refs)
    ]
    loads = [
        pltpu.make_async_copy(src, dst, load_sem.at[place])
        for place, (src, dst) in enumerate(
            [(rope_hbm, rope), (ku_hbm, ku)] + lat_parts + [(vu_hbm, vu_ref)]
        )
    ]
    for copy in own:
        copy.start()
    for copy in loads:
        copy.start()
    greet(count, me)

    def held(part, owner):
        return qr_all.at[owner] if part == groups else qn_all.at[part, owner]

    def along(part, step):
        peer = lax.rem(line + step, outer) * 2 + side
        return remote(
            held(part, me), held(part, me), send_z.at[part, step], recv_z.at[part, step], peer
        )

    def across(part, step):
        owner = lax.rem(line + outer - step, outer) * 2 + side
        return remote(
            held(part, owner), held(part, owner), send_x.at[part, step], recv_x.at[part, step],
            partner,
        )

    for part in range(groups + 1):
        own[part].wait()
        for step in range(1, outer):
            along(part, step).start()
        across(part, 0).start()

    def forward(part):
        for step in range(1, outer):
            along(part, step).wait_recv()
            across(part, step).start()

    loads[0].wait()
    low_key = lax.broadcasted_iota(jnp.int32, (blocks, LANES), 1) < rope_width

    def spread(pair, carry):
        lanes = pl.ds(pl.multiple_of(pair * LANES, LANES), LANES)
        chunk = rope[:, lanes].astype(jnp.float32)
        keys[pl.ds(2 * pair, blocks, stride=width), :] = jnp.where(low_key, chunk, 0.0)
        keys[pl.ds(2 * pair + 1, blocks, stride=width), :] = jnp.where(low_key, 0.0, chunk)
        return carry

    lax.fori_loop(0, width // 2, spread, 0, unroll=4)
    forward(0)

    def settle(block, carry):
        rows = pl.ds(pl.multiple_of(block * width, width), width)
        key_ref[rows, :] = keys[rows, :].astype(jnp.bfloat16)
        return carry

    lax.fori_loop(0, blocks, settle, 0, unroll=2)
    loads[1].wait()
    batch = 4
    for part in range(groups):
        forward(part + 1)
        for step in range(outer):
            across(part, step).wait_recv()
        for source in range(count):
            rows = pl.ds(source * row_part, row_part)
            qn_wide[rows, part * span : (part + 1) * span] = qn_all[part, source].astype(
                jnp.float32
            )

        def one_batch(turn, carry):
            for inner in range(batch):
                head = part * group_heads + turn * batch + inner
                lanes = pl.ds(pl.multiple_of(head * LANES, LANES), LANES)
                query = qn_wide[:, lanes].astype(jnp.bfloat16)
                result = jnp.dot(query, ku[head], preferred_element_type=jnp.float32)
                for tile in range(latent_tiles):
                    q_wide[tile, pl.ds(head, rows_all, stride=heads), :] = result[
                        :, tile * LANES : (tile + 1) * LANES
                    ]
            return carry

        lax.fori_loop(0, group_heads // batch, one_batch, 0)
    for step in range(outer):
        across(groups, step).wait_recv()
    for source in range(count):
        qr_wide[pl.ds(source * row_part, row_part), :] = qr_all[source].astype(jnp.float32)
    low = lax.broadcasted_iota(jnp.int32, (rows_all, LANES), 1) < rope_width
    for pair in range(heads // 2):
        chunk = qr_wide[:, pair * LANES : (pair + 1) * LANES]
        turned = pltpu.roll(chunk, rope_width, 1)
        q_wide[latent_tiles, pl.ds(2 * pair, rows_all, stride=heads), :] = jnp.where(
            low, chunk, turned
        )
        q_wide[latent_tiles, pl.ds(2 * pair + 1, rows_all, stride=heads), :] = jnp.where(
            low, turned, chunk
        )
    for tile in range(latent_tiles + 1):
        q_ref[:, tile * LANES : (tile + 1) * LANES] = q_wide[tile].astype(jnp.bfloat16)
    for part in range(groups + 1):
        across(part, 0).wait_send()
        for step in range(1, outer):
            along(part, step).wait_send()
            across(part, step).wait_send()
    for copy in loads[2:]:
        copy.wait()


def attend_kernel(
    count, heads, groups, new_tokens, lengths, owners, numbers, q_ref, lat_a, lat_b, lat_c, lat_d,
    keys, accum, inverse_ref, stat_ref, scores, tops, totals,
):
    lat_refs = (lat_a, lat_b, lat_c, lat_d)
    quarter, width, latent_width = lat_a.shape
    blocks = quarter * len(lat_refs)
    latent_tiles = latent_width // LANES
    seq_rows = new_tokens * heads
    queries = q_ref.shape[0]
    dest_rows = queries // count
    per_set = 8
    sets = quarter // per_set
    tops[...] = jnp.full(tops.shape, floor_value, jnp.float32)
    totals[...] = jnp.zeros(totals.shape, jnp.float32)
    accum[...] = jnp.zeros(accum.shape, jnp.float32)
    token = lax.broadcasted_iota(jnp.int32, (seq_rows, width), 0) // heads
    slot = lax.broadcasted_iota(jnp.int32, (seq_rows, width), 1)
    offset = slot - token
    contract_last = (((1,), (1,)), ((), ()))

    def score_one(block, latent):
        owner = owners[block]
        safe = jnp.maximum(owner, 0)
        rows = pl.ds(pl.multiple_of(safe * seq_rows, seq_rows), seq_rows)
        low_key = keys[pl.ds(pl.multiple_of(block * width, width), width), :]
        logits = lax.dot_general(
            q_ref[rows, :latent_width], latent, contract_last,
            preferred_element_type=jnp.float32,
        ) + lax.dot_general(
            q_ref[rows, latent_width:], low_key, contract_last, preferred_element_type=jnp.float32
        )
        limit = lengths[safe] - (new_tokens - 1) - numbers[block] * width
        limit = jnp.where(owner >= 0, limit, -width)
        logits = jnp.where(offset < limit, logits * score_scale, floor_value)
        return rows, logits

    for place, lat in enumerate(lat_refs):

        def score_set(part, carry):
            for inner in range(per_set):
                near = part * per_set + inner
                block = place * quarter + near
                rows, logits = score_one(block, lat[near])
                scores[block] = logits
                tops[rows, :] = jnp.maximum(tops[rows, :], logits)
            return carry

        lax.fori_loop(0, sets, score_set, 0)
    for row in range(0, queries, seq_rows):
        rows = pl.ds(row, seq_rows)
        top = jnp.max(tops[rows, :], axis=1, keepdims=True)
        tops[rows, :] = jnp.broadcast_to(jnp.maximum(top, 0.1 * floor_value), (seq_rows, LANES))

    for place, lat in enumerate(lat_refs):

        def weigh_set(part, carry):
            for inner in range(per_set):
                near = part * per_set + inner
                block = place * quarter + near
                safe = jnp.maximum(owners[block], 0)
                rows = pl.ds(pl.multiple_of(safe * seq_rows, seq_rows), seq_rows)
                weight = jnp.exp(scores[block] - tops[rows, :])
                totals[rows, :] += weight
                part_accum = jnp.dot(
                    weight.astype(jnp.bfloat16), lat[near], preferred_element_type=jnp.float32
                )
                for tile in range(latent_tiles):
                    accum[tile, rows, :] += part_accum[:, tile * LANES : (tile + 1) * LANES]
            return carry

        lax.fori_loop(0, sets, weigh_set, 0)
    group_heads = heads // groups
    for dest in range(count):
        rows = pl.ds(dest * dest_rows, dest_rows)
        total = jnp.sum(totals[rows, :], axis=1, keepdims=True)
        held = total > 0.0
        safe_total = jnp.where(held, total, 1.0)
        mass = jnp.where(held, tops[rows, :] + jnp.log(safe_total), floor_value)
        inverse_ref[rows, :] = jnp.broadcast_to(1.0 / safe_total, (dest_rows, LANES))
        ordered = jnp.concatenate(
            [
                mass[first : first + group_heads]
                for part in range(groups)
                for first in range(part * group_heads, dest_rows, heads)
            ],
            axis=0,
        )
        stat_ref[dest] = jnp.transpose(ordered)[:1, :]


def merge_kernel(
    count, groups, accum, inverse, stat_ref, vu, result_ref, values, sent, outs, stats, merged,
    send_a, recv_a, send_b, recv_b, own_sem,
):
    me = lax.axis_index("ctx")
    row_part = result_ref.shape[0]
    heads = vu.shape[0]
    latent_tiles = accum.shape[0]
    queries = accum.shape[1]
    rows_all = queries // heads
    group_heads = heads // groups
    group_rows = row_part * group_heads
    own_stat = pltpu.make_async_copy(stat_ref.at[me], stats.at[me], own_sem.at[groups])
    own_stat.start()
    greet(count, me)
    copies = [[] for part in range(groups + 1)]
    for step in range(1, count):
        peer = lax.rem(me + step, count)
        copy = remote(
            stat_ref.at[peer], stats.at[me], send_b.at[step], recv_b.at[step], peer
        )
        copy.start()
        copies[groups].append(copy)
    for part in range(groups):

        def lift(head, carry):
            picked = pl.ds(part * group_heads + head, rows_all, stride=heads)
            whole = jnp.concatenate(
                [accum[tile, picked, :].astype(jnp.bfloat16) for tile in range(latent_tiles)],
                axis=1,
            )
            lifted = jnp.dot(
                whole, vu[part * group_heads + head], preferred_element_type=jnp.float32
            )
            values[pl.ds(head, rows_all, stride=group_heads), :] = lifted * inverse[picked, :]
            return carry

        lax.fori_loop(0, group_heads, lift, 0, unroll=4)
        for dest in range(count):
            rows = pl.ds(dest * group_rows, group_rows)
            sent[part, dest] = values[rows, :].astype(jnp.bfloat16)
        own_part = pltpu.make_async_copy(
            sent.at[part, me], outs.at[part, me], own_sem.at[part]
        )
        own_part.start()
        copies[part].append(own_part)
        for step in range(1, count):
            peer = lax.rem(me + step, count)
            copy = remote(
                sent.at[part, peer], outs.at[part, me], send_a.at[part, step],
                recv_a.at[part, step], peer,
            )
            copy.start()
            copies[part].append(copy)
    own_stat.wait()
    for copy in copies[groups]:
        copy.wait()
    mass = jnp.transpose(stats[:, 0, :])
    share = jnp.exp(mass - jnp.max(mass, axis=1, keepdims=True))
    share = share * (1.0 / jnp.sum(share, axis=1, keepdims=True))
    for part in range(groups):
        for copy in copies[part]:
            copy.wait()
        total = None
        for source in range(count):
            piece = share[
                part * group_rows : (part + 1) * group_rows, source : source + 1
            ] * outs[part, source].astype(jnp.float32)
            total = piece if total is None else total + piece
        merged[...] = total
        for head in range(group_heads):
            first = (part * group_heads + head) * LANES
            result_ref[:, first : first + LANES] = merged[
                pl.ds(head, row_part, stride=group_heads), :
            ].astype(jnp.bfloat16)


def per_device(
    query_nope, query_rope, cache_latent, cache_rope, key_up, value_up, lengths, block_owner,
    block_number,
):
    count = lax.axis_size("ctx")
    row_part = query_nope.shape[0]
    heads, nope_width, latent_width = key_up.shape
    value_width = value_up.shape[2]
    rows_all = row_part * count
    new_tokens = rows_all // lengths.shape[0]
    blocks, width, _ = cache_latent.shape
    queries = rows_all * heads
    q_width = latent_width + LANES
    latent_tiles = latent_width // LANES
    dest_rows = row_part * heads
    groups = max(1, heads // count)
    group_heads = heads // groups
    outer = count // 2
    vmem = pl.BlockSpec(memory_space=pltpu.VMEM)
    smem = pl.BlockSpec(memory_space=pltpu.SMEM)
    hbm = pl.BlockSpec(memory_space=pltpu.HBM)
    dma = pltpu.SemaphoreType.DMA
    f32, bf16 = jnp.float32, jnp.bfloat16
    mib = 1024 * 1024
    quarter_shape = (blocks // 4,) + cache_latent.shape[1:]
    query, *latents, keys, lifts = pl.pallas_call(
        functools.partial(absorb_kernel, count, groups),
        name="absorb",
        out_shape=(
            jax.ShapeDtypeStruct((queries, q_width), bf16),
            *[jax.ShapeDtypeStruct(quarter_shape, bf16)] * 4,
            jax.ShapeDtypeStruct((blocks * width, LANES), bf16),
            jax.ShapeDtypeStruct(value_up.shape, bf16),
        ),
        in_specs=[hbm] * 6,
        out_specs=(vmem,) * 7,
        scratch_shapes=[
            pltpu.VMEM((groups, count, row_part, group_heads * nope_width), bf16),
            pltpu.VMEM((count,) + query_rope.shape, bf16),
            pltpu.VMEM((rows_all, query_nope.shape[1]), f32),
            pltpu.VMEM((rows_all, query_rope.shape[1]), f32),
            pltpu.VMEM((latent_tiles + 1, queries, LANES), f32),
            pltpu.VMEM(key_up.shape, bf16),
            pltpu.VMEM(cache_rope.shape, bf16),
            pltpu.VMEM((blocks * width, LANES), f32),
            dma((groups + 1, outer)), dma((groups + 1, outer)),
            dma((groups + 1, outer)), dma((groups + 1, outer)),
            dma((groups + 1,)), dma((7,)),
        ],
        compiler_params=pltpu.CompilerParams(
            collective_id=0, has_side_effects=True, vmem_limit_bytes=38_500_000
        ),
    )(query_nope, query_rope, key_up, cache_latent, cache_rope, value_up)
    accum, inverse, stats = pl.pallas_call(
        functools.partial(attend_kernel, count, heads, groups, new_tokens),
        name="attend",
        out_shape=(
            jax.ShapeDtypeStruct((latent_tiles, queries, LANES), f32),
            jax.ShapeDtypeStruct((queries, LANES), f32),
            jax.ShapeDtypeStruct((count, 1, dest_rows), f32),
        ),
        in_specs=[smem] * 3 + [vmem] * 6,
        out_specs=(vmem,) * 3,
        scratch_shapes=[
            pltpu.VMEM((blocks, new_tokens * heads, width), f32),
            pltpu.VMEM((queries, LANES), f32),
            pltpu.VMEM((queries, LANES), f32),
        ],
        compiler_params=pltpu.CompilerParams(vmem_limit_bytes=24 * mib),
    )(lengths, block_owner, block_number, query, *latents, keys)
    return pl.pallas_call(
        functools.partial(merge_kernel, count, groups),
        name="merge",
        out_shape=jax.ShapeDtypeStruct((row_part, heads * value_width), bf16),
        in_specs=[vmem] * 4,
        out_specs=vmem,
        scratch_shapes=[
            pltpu.VMEM((rows_all * group_heads, LANES), f32),
            pltpu.VMEM((groups, count, row_part * group_heads, value_width), bf16),
            pltpu.VMEM((groups, count, row_part * group_heads, value_width), bf16),
            pltpu.VMEM((count, 1, dest_rows), f32),
            pltpu.VMEM((row_part * group_heads, LANES), f32),
            dma((groups, count)), dma((groups, count)), dma((count,)), dma((count,)),
            dma((groups + 1,)),
        ],
        compiler_params=pltpu.CompilerParams(
            collective_id=1, has_side_effects=True, vmem_limit_bytes=16 * mib
        ),
    )(accum, inverse, stats, lifts)


def solution(mesh):
    return jax.shard_map(
        per_device,
        mesh=mesh,
        in_specs=(
            P("ctx", "head"),
            P("ctx", "head"),
            P("ctx", None, None),
            P("ctx", None),
            P("head", None, None),
            P("head", None, None),
            P(),
            P("ctx"),
            P("ctx"),
        ),
        out_specs=P("ctx", "head"),
        check_vma=False,
    )
```

time: 50.3 us -> 44.9 us (0.89)
  Pallas kernels: 45.7 us -> 41.3 us
  local copies, waits for them, and re-layouts: 4.29 us -> 3.33 us
    pallas_call x3, Pallas kernels: 45.7 us -> 41.3 us  [the longest x1 21.7 us: per_device(): pl.pallas_call(functools.partial(absorb_kernel, count, groups), name='abs...]
    unnamed x15 -> x13, local copies, waits for them, and re-layouts: 4.29 us -> 3.33 us
where the time goes in v2:
time: 44.9 us; the launch traced here: 44.7 us
  Pallas kernels  41.3 us (92%)
  local copies, waits for them, and re-layouts  3.33 us (7%)
    pallas_call x1, Pallas kernels, per_device(): pl.pallas_call(functools.partial(absorb_kernel, count, groups), name='abs...  21.7 us
    pallas_call x1, Pallas kernels, per_device(): pl.pallas_call(functools.partial(merge_kernel, count, groups), name='merg...  10.6 us
    pallas_call x1, Pallas kernels, per_device(): pl.pallas_call(functools.partial(attend_kernel, count, heads, groups, new...  8.99 us
    unnamed x13, local copies, waits for them, and re-layouts  3.33 us

profile of v2, /device:TPU:0, one launch (start us, length us, event | category | flops | bytes accessed | tf_op | source)
XLA Modules:
  0.0 44.7 jit_solution(5274909619842894264)
XLA Ops:
  0.0 0.0 copy-start
  0.0 1.2 %copy-done = bf16[64,8192]{1,0:T(8,128)(2,1)S(1)} copy-done((bf16[64,8192]{1,0:T(8,128)(2,1)S(1)}, bf16[64,8192]{1,0:T(8,128)(2,1)}, u32[]{:S(2)}) %copy-start) | copy-done | bytes 1048600
  1.2 0.0 copy-start.1
  1.2 0.8 %copy-done.1 = bf16[4,4096]{1,0:T(4,128)(2,1)S(1)} copy-done((bf16[4,4096]{1,0:T(4,128)(2,1)S(1)}, bf16[4,4096]{1,0:T(4,128)(2,1)}, u32[]{:S(2)}) %copy-start.1) | copy-done | bytes 32792
  2.0 0.0 copy-start.2
  2.0 0.7 %copy-done.2 = bf16[4,2048]{1,0:T(4,128)(2,1)S(1)} copy-done((bf16[4,2048]{1,0:T(4,128)(2,1)S(1)}, bf16[4,2048]{1,0:T(4,128)(2,1)}, u32[]{:S(2)}) %copy-start.2) | copy-done | bytes 16408
  2.7 0.0 copy-start.3
  2.7 0.0 copy-start.4
  2.7 0.0 copy-start.5
  2.7 21.7 %absorb.1 = (bf16[1024,640]{1,0:T(8,128)(2,1)S(1)}, bf16[16,128,512]{2,1,0:T(8,128)(2,1)S(1)}, bf16[16,128,512]{2,1,0:T(8,128)(2,1)S(1)}, bf16[16,128,512]{2,1,0...) custom-call(bf16[4,4096]{1,0:T(4,128)(2,1)S(1)} %copy-done.1, ...), custom_call_target="tpu_custom_call" | custom-call | tf_op jit(solution)/shard_map/absorb/pallas_call | solution.py:362
  24.4 0.0 copy-done.3
  24.4 0.0 copy-done.4
  24.4 0.0 copy-done.5
  24.4 9.0 %attend.1 = (f32[4,1024,128]{2,1,0:T(8,128)S(1)}, f32[1024,128]{1,0:T(8,128)S(1)}, f32[8,1,128]{2,1,0:T(1,128)S(1)}) custom-call(s32[16]{0:T(128)S(1)} %copy-done.3, s32[64]{0:T(128)S(1)} %copy-done.4, s32[64]{0:T(128)S(1)} %copy-done.5, bf16[1024,640]{1,0:T(8,128)(2,1)S(1)} %get-tuple-element.15.q_ref, bf16[16,128,512]{2,1,0:T(8,128)(2,1)S(1)} %get-tuple-element.16.lat_a, ...), custom_call_target="tpu_custom_call" | custom-call | tf_op jit(solution)/shard_map/attend/pallas_call | solution.py:390
  33.4 10.6 %merge.1 = bf16[4,4096]{1,0:T(4,128)(2,1)S(1)} custom-call(f32[4,1024,128]{2,1,0:T(8,128)S(1)} %get-tuple-element.21.accum, f32[1024,128]{1,0:T(8,128)S(1)} %get-tuple-element.22.inverse, f32[8,1,128]{2,1,0:T(1,128)S(1)} %get-tuple-element.23.stat_ref, bf16[32,512,128]{2,1,0:T(8,128)(2,1)S(1)} %get-tuple-element.24.vu), custom_call_target="tpu_custom_call" | custom-call | tf_op jit(solution)/shard_map/merge/pallas_call | solution.py:407
  44.0 0.6 %copy.11 = bf16[4,4096]{1,0:T(4,128)(2,1)} copy(bf16[4,4096]{1,0:T(4,128)(2,1)S(1)} %merge.1) | data formatting | bytes 65536
Async XLA Ops:
  0.0 1.2 %copy-start = (bf16[64,8192]{1,0:T(8,128)(2,1)S(1)}, bf16[64,8192]{1,0:T(8,128)(2,1)}, u32[]{:S(2)}) copy-start(bf16[64,8192]{1,0:T(8,128)(2,1)} %rope_hbm.1) | copy-start | bytes 3145732
  1.2 0.8 %copy-start.1 = (bf16[4,4096]{1,0:T(4,128)(2,1)S(1)}, bf16[4,4096]{1,0:T(4,128)(2,1)}, u32[]{:S(2)}) copy-start(bf16[4,4096]{1,0:T(4,128)(2,1)} %qn_hbm.1) | copy-start | bytes 98308
  2.0 0.7 %copy-start.2 = (bf16[4,2048]{1,0:T(4,128)(2,1)S(1)}, bf16[4,2048]{1,0:T(4,128)(2,1)}, u32[]{:S(2)}) copy-start(bf16[4,2048]{1,0:T(4,128)(2,1)} %qr_hbm.1) | copy-start | bytes 49156
  2.7 21.7 %copy-start.3 = (s32[16]{0:T(128)S(1)}, s32[16]{0:T(128)}, u32[]{:S(2)}) copy-start(s32[16]{0:T(128)} %lengths.1) | copy-start | bytes 196
  2.7 21.7 %copy-start.4 = (s32[64]{0:T(128)S(1)}, s32[64]{0:T(128)}, u32[]{:S(2)}) copy-start(s32[64]{0:T(128)} %owners.1) | copy-start | bytes 772
  2.7 21.7 %copy-start.5 = (s32[64]{0:T(128)S(1)}, s32[64]{0:T(128)}, u32[]{:S(2)}) copy-start(s32[64]{0:T(128)} %numbers.1) | copy-start | bytes 772

commit v3 on v2

--- a/solution.py
+++ b/solution.py
@@ -32,12 +32,9 @@
 def absorb_kernel(
     count, groups, qn_hbm, qr_hbm, ku_hbm, lat_hbm, rope_hbm, vu_hbm, q_ref, lat_a, lat_b,
     lat_c, lat_d, key_ref, vu_ref, qn_all, qr_all, qn_wide, qr_wide, q_wide, ku, rope, keys,
-    send_z, recv_z, send_x, recv_x, own_sem, load_sem,
+    send_z, recv_z, own_sem, load_sem,
 ):
     me = lax.axis_index("ctx")
-    outer = count // 2
-    line, side = me // 2, lax.rem(me, 2)
-    partner = me + 1 - 2 * side
     heads = ku.shape[0]
     latent_tiles = ku.shape[2] // LANES
     row_part = qn_hbm.shape[0]
@@ -73,29 +70,16 @@
     def held(part, owner):
         return qr_all.at[owner] if part == groups else qn_all.at[part, owner]
 
-    def along(part, step):
-        peer = lax.rem(line + step, outer) * 2 + side
+    def direct(part, step):
         return remote(
-            held(part, me), held(part, me), send_z.at[part, step], recv_z.at[part, step], peer
-        )
-
-    def across(part, step):
-        owner = lax.rem(line + outer - step, outer) * 2 + side
-        return remote(
-            held(part, owner), held(part, owner), send_x.at[part, step], recv_x.at[part, step],
-            partner,
+            held(part, me), held(part, me), send_z.at[part, step], recv_z.at[part, step],
+            lax.rem(me + step, count),
         )
 
     for part in range(groups + 1):
         own[part].wait()
-        for step in range(1, outer):
-            along(part, step).start()
-        across(part, 0).start()
-
-    def forward(part):
-        for step in range(1, outer):
-            along(part, step).wait_recv()
-            across(part, step).start()
+        for step in range(1, count):
+            direct(part, step).start()
 
     loads[0].wait()
     low_key = lax.broadcasted_iota(jnp.int32, (blocks, LANES), 1) < rope_width
@@ -108,7 +92,6 @@
         return carry
 
     lax.fori_loop(0, width // 2, spread, 0, unroll=4)
-    forward(0)
 
     def settle(block, carry):
         rows = pl.ds(pl.multiple_of(block * width, width), width)
@@ -119,9 +102,8 @@
     loads[1].wait()
     batch = 4
     for part in range(groups):
-        forward(part + 1)
-        for step in range(outer):
-            across(part, step).wait_recv()
+        for step in range(1, count):
+            direct(part, step).wait_recv()
         for source in range(count):
             rows = pl.ds(source * row_part, row_part)
             qn_wide[rows, part * span : (part + 1) * span] = qn_all[part, source].astype(
@@ -141,8 +123,8 @@
             return carry
 
         lax.fori_loop(0, group_heads // batch, one_batch, 0)
-    for step in range(outer):
-        across(groups, step).wait_recv()
+    for step in range(1, count):
+        direct(groups, step).wait_recv()
     for source in range(count):
         qr_wide[pl.ds(source * row_part, row_part), :] = qr_all[source].astype(jnp.float32)
     low = lax.broadcasted_iota(jnp.int32, (rows_all, LANES), 1) < rope_width
@@ -158,10 +140,8 @@
     for tile in range(latent_tiles + 1):
         q_ref[:, tile * LANES : (tile + 1) * LANES] = q_wide[tile].astype(jnp.bfloat16)
     for part in range(groups + 1):
-        across(part, 0).wait_send()
-        for step in range(1, outer):
-            along(part, step).wait_send()
-            across(part, step).wait_send()
+        for step in range(1, count):
+            direct(part, step).wait_send()
     for copy in loads[2:]:
         copy.wait()
 
@@ -351,7 +331,6 @@
     dest_rows = row_part * heads
     groups = max(1, heads // count)
     group_heads = heads // groups
-    outer = count // 2
     vmem = pl.BlockSpec(memory_space=pltpu.VMEM)
     smem = pl.BlockSpec(memory_space=pltpu.SMEM)
     hbm = pl.BlockSpec(memory_space=pltpu.HBM)
@@ -379,8 +358,7 @@
             pltpu.VMEM(key_up.shape, bf16),
             pltpu.VMEM(cache_rope.shape, bf16),
             pltpu.VMEM((blocks * width, LANES), f32),
-            dma((groups + 1, outer)), dma((groups + 1, outer)),
-            dma((groups + 1, outer)), dma((groups + 1, outer)),
+            dma((groups + 1, count)), dma((groups + 1, count)),
             dma((groups + 1,)), dma((7,)),
         ],
         compiler_params=pltpu.CompilerParams(

time: 44.9 us -> 40.8 us (0.909)
  Pallas kernels: 41.3 us -> 37.2 us
    pallas_call x1, Pallas kernels: 21.7 us -> 16.5 us  [per_device(): pl.pallas_call(functools.partial(absorb_kernel, count, groups), name='abs...]
    pallas_call x1, Pallas kernels: 10.6 us -> 11.7 us  [per_device(): pl.pallas_call(functools.partial(merge_kernel, count, groups), name='merg...]
where the time goes in v3:
time: 40.8 us; the launch traced here: 40.6 us
  Pallas kernels  37.2 us (91%)
  local copies, waits for them, and re-layouts  3.33 us (8%)
    pallas_call x1, Pallas kernels, per_device(): pl.pallas_call(functools.partial(absorb_kernel, count, groups), name='abs...  16.5 us
    pallas_call x1, Pallas kernels, per_device(): pl.pallas_call(functools.partial(merge_kernel, count, groups), name='merg...  11.7 us
    pallas_call x1, Pallas kernels, per_device(): pl.pallas_call(functools.partial(attend_kernel, count, heads, groups, new...  9 us
    unnamed x13, local copies, waits for them, and re-layouts  3.33 us

profile of v3, /device:TPU:0, one launch (start us, length us, event | category | flops | bytes accessed | tf_op | source)
XLA Modules:
  0.0 40.6 jit_solution(18318268121663159950)
XLA Ops:
  0.0 0.0 copy-start
  0.0 1.2 %copy-done = bf16[64,8192]{1,0:T(8,128)(2,1)S(1)} copy-done((bf16[64,8192]{1,0:T(8,128)(2,1)S(1)}, bf16[64,8192]{1,0:T(8,128)(2,1)}, u32[]{:S(2)}) %copy-start) | copy-done | bytes 1048600
  1.2 0.0 copy-start.1
  1.2 0.8 %copy-done.1 = bf16[4,4096]{1,0:T(4,128)(2,1)S(1)} copy-done((bf16[4,4096]{1,0:T(4,128)(2,1)S(1)}, bf16[4,4096]{1,0:T(4,128)(2,1)}, u32[]{:S(2)}) %copy-start.1) | copy-done | bytes 32792
  2.0 0.0 copy-start.2
  2.0 0.7 %copy-done.2 = bf16[4,2048]{1,0:T(4,128)(2,1)S(1)} copy-done((bf16[4,2048]{1,0:T(4,128)(2,1)S(1)}, bf16[4,2048]{1,0:T(4,128)(2,1)}, u32[]{:S(2)}) %copy-start.2) | copy-done | bytes 16408
  2.7 0.0 copy-start.3
  2.7 0.0 copy-start.4
  2.7 0.0 copy-start.5
  2.7 16.5 %absorb.1 = (bf16[1024,640]{1,0:T(8,128)(2,1)S(1)}, bf16[16,128,512]{2,1,0:T(8,128)(2,1)S(1)}, bf16[16,128,512]{2,1,0:T(8,128)(2,1)S(1)}, bf16[16,128,512]{2,1,0...) custom-call(bf16[4,4096]{1,0:T(4,128)(2,1)S(1)} %copy-done.1, ...), custom_call_target="tpu_custom_call" | custom-call | tf_op jit(solution)/shard_map/absorb/pallas_call | solution.py:341
  19.2 0.0 copy-done.3
  19.2 0.0 copy-done.4
  19.2 0.0 copy-done.5
  19.2 9.0 %attend.1 = (f32[4,1024,128]{2,1,0:T(8,128)S(1)}, f32[1024,128]{1,0:T(8,128)S(1)}, f32[8,1,128]{2,1,0:T(1,128)S(1)}) custom-call(s32[16]{0:T(128)S(1)} %copy-done.3, s32[64]{0:T(128)S(1)} %copy-done.4, s32[64]{0:T(128)S(1)} %copy-done.5, bf16[1024,640]{1,0:T(8,128)(2,1)S(1)} %get-tuple-element.15.q_ref, bf16[16,128,512]{2,1,0:T(8,128)(2,1)S(1)} %get-tuple-element.16.lat_a, ...), custom_call_target="tpu_custom_call" | custom-call | tf_op jit(solution)/shard_map/attend/pallas_call | solution.py:368
  28.2 11.7 %merge.1 = bf16[4,4096]{1,0:T(4,128)(2,1)S(1)} custom-call(f32[4,1024,128]{2,1,0:T(8,128)S(1)} %get-tuple-element.21.accum, f32[1024,128]{1,0:T(8,128)S(1)} %get-tuple-element.22.inverse, f32[8,1,128]{2,1,0:T(1,128)S(1)} %get-tuple-element.23.stat_ref, bf16[32,512,128]{2,1,0:T(8,128)(2,1)S(1)} %get-tuple-element.24.vu), custom_call_target="tpu_custom_call" | custom-call | tf_op jit(solution)/shard_map/merge/pallas_call | solution.py:385
  39.9 0.6 %copy.11 = bf16[4,4096]{1,0:T(4,128)(2,1)} copy(bf16[4,4096]{1,0:T(4,128)(2,1)S(1)} %merge.1) | data formatting | bytes 65536
Async XLA Ops:
  0.0 1.2 %copy-start = (bf16[64,8192]{1,0:T(8,128)(2,1)S(1)}, bf16[64,8192]{1,0:T(8,128)(2,1)}, u32[]{:S(2)}) copy-start(bf16[64,8192]{1,0:T(8,128)(2,1)} %rope_hbm.1) | copy-start | bytes 3145732
  1.2 0.8 %copy-start.1 = (bf16[4,4096]{1,0:T(4,128)(2,1)S(1)}, bf16[4,4096]{1,0:T(4,128)(2,1)}, u32[]{:S(2)}) copy-start(bf16[4,4096]{1,0:T(4,128)(2,1)} %qn_hbm.1) | copy-start | bytes 98308
  2.0 0.7 %copy-start.2 = (bf16[4,2048]{1,0:T(4,128)(2,1)S(1)}, bf16[4,2048]{1,0:T(4,128)(2,1)}, u32[]{:S(2)}) copy-start(bf16[4,2048]{1,0:T(4,128)(2,1)} %qr_hbm.1) | copy-start | bytes 49156
  2.7 16.5 %copy-start.3 = (s32[16]{0:T(128)S(1)}, s32[16]{0:T(128)}, u32[]{:S(2)}) copy-start(s32[16]{0:T(128)} %lengths.1) | copy-start | bytes 196
  2.7 16.5 %copy-start.4 = (s32[64]{0:T(128)S(1)}, s32[64]{0:T(128)}, u32[]{:S(2)}) copy-start(s32[64]{0:T(128)} %owners.1) | copy-start | bytes 772
  2.7 16.5 %copy-start.5 = (s32[64]{0:T(128)S(1)}, s32[64]{0:T(128)}, u32[]{:S(2)}) copy-start(s32[64]{0:T(128)} %numbers.1) | copy-start | bytes 772
